TPU v7x, 32 devices: a whole 2x2x4 slice. The times are simulated.
32 devices in a mesh: group: 2 (over y), station: 4 (over z), tm: 2 (over x), chan: 2 (over core).
Axes of the slice: x: 2, y: 2, z: 4, core: 2. Of those that a mesh axis runs over, the one named last changes fastest.
Arguments:
- voltages: bfloat16 [8, 128, 2, 96, 256], P(('group', 'station'), 'chan', None, None, 'tm'), parts along dimension 0, may hold values from -6 to 6
- delays: int32 [8], P(('group', 'station')), parts along dimension 0, may hold values from 0 to 16, as said below
- tap_sets: int32 [8, 128], P(('group', 'station'), 'chan'), parts along dimension 0, may hold values from 0 to 15
- tap_table: bfloat16 [16, 16], replicated, may hold values from -1.5 to 1.5
- weights: bfloat16 [8, 128, 2, 96, 128], P(('group', 'station'), 'chan'), parts along dimension 0, may hold values from -0.3125 to 0.3125
Outputs:
- array_beams: bfloat16 [256, 2, 128, 256], P(('group', 'chan', 'station'), None, None, 'tm'), parts along dimension 0
There are 2 independent parts, one for each index of `group`. A program takes and returns all parts, laid end to end along the dimension named above; an argument that names none is the same for every part. Nothing has to cross between parts.
Inputs may be any that keep to these rules, and one draw needn't show every extreme that they name: `delays`: every delay lies in 0 to 16, and some station has delay 16.
All inputs are finite; a program needn't handle non-finite values.
Results may differ from a plain program's by a relative error of at most 0.0049.
Values may be sent and summed in bfloat16 or wider, within the bound.
A program may use at most 64 MiB of HBM per device.

v0:
```python
import jax
import jax.numpy as jnp
from jax import lax
from jax.sharding import PartitionSpec as P

TAPS = 16
MAXD = 16
BLOCK = 128


def passed_along(value, axis, steps):
    count = lax.axis_size(axis)
    leading, last = (max(0, -steps), min(count, count - steps))
    return lax.ppermute(value, axis, [(source, source + steps) for source in range(leading, last)])


def steering_matrix(weights):
    real_w = weights[:, :, 0]
    imag_w = weights[:, :, 1]
    upper_rows = jnp.concatenate([real_w, imag_w], axis=-1)
    lower_rows = jnp.concatenate([-imag_w, real_w], axis=-1)
    return jnp.concatenate([upper_rows, lower_rows], axis=2)


def body(voltages, delays, tap_sets, tap_table, weights):
    station_number, channel_total, pairing_total, antenna_total, time_length = voltages.shape
    set_count, tap_count = tap_table.shape
    halo_len = MAXD + TAPS - 1
    window_len = BLOCK + halo_len
    flat_voltages = voltages.reshape(
        station_number, channel_total, pairing_total * antenna_total, time_length
    )
    prev_rim = passed_along(flat_voltages[..., time_length - halo_len :], "tm", 1)
    extended = jnp.concatenate([prev_rim, flat_voltages], axis=-1)
    windows = jnp.stack([extended], axis=3)
    set_onehot = (tap_sets[..., None] == jnp.arange(set_count)[None, None, :]).astype(jnp.bfloat16)
    chosen_taps = jnp.einsum(
        "scm,mk->sck", set_onehot, tap_table, preferred_element_type=jnp.float32
    ).astype(jnp.bfloat16)
    window_pos = jnp.arange(window_len)[:, None]
    output_pos = jnp.arange(BLOCK)[None, :]
    lag_table = output_pos + halo_len - window_pos
    station_lag = lag_table[None, :, :] - delays[:, None, None]
    tap_onehot = (station_lag[..., None] == jnp.arange(tap_count)[None, None, None, :]).astype(
        jnp.bfloat16
    )
    band_matrix = jnp.einsum(
        "sck,sjuk->scju", chosen_taps, tap_onehot, preferred_element_type=jnp.float32
    ).astype(jnp.bfloat16)
    delayed_voltages = jnp.einsum(
        "scanj,scju->scanu", windows, band_matrix, preferred_element_type=jnp.float32
    ).astype(jnp.bfloat16)
    delayed_voltages = delayed_voltages.reshape(
        station_number, channel_total, pairing_total * antenna_total, time_length
    )
    station_axis_size = lax.axis_size("station")
    row_count = channel_total // station_axis_size
    split_in = delayed_voltages.reshape(
        station_number, station_axis_size, row_count, pairing_total * antenna_total, time_length
    )
    split_steer = weights.reshape(
        station_number,
        station_axis_size,
        row_count,
        pairing_total,
        antenna_total,
        weights.shape[-1],
    )
    gathered_in = lax.all_to_all(split_in, "station", split_axis=1, concat_axis=0, tiled=True)
    gathered_w = lax.all_to_all(split_steer, "station", split_axis=1, concat_axis=0, tiled=True)
    summed = jnp.einsum(
        "scan,scat->cnt",
        steering_matrix(gathered_w[:, 0]),
        gathered_in[:, 0],
        preferred_element_type=jnp.float32,
    )
    beam_count = weights.shape[-1]
    return summed.astype(jnp.bfloat16).reshape(row_count, 2, beam_count, time_length)


def solution(mesh):
    return jax.shard_map(
        body,
        mesh=mesh,
        in_specs=(
            P(("group", "station"), "chan", None, None, "tm"),
            P(("group", "station")),
            P(("group", "station"), "chan"),
            P(),
            P(("group", "station"), "chan", None, None, None),
        ),
        out_specs=P(("group", "chan", "station"), None, None, "tm"),
        check_vma=False,
    )
```

profile of v0, /device:TPU:0, one launch (start us, length us, event | category | flops | bytes accessed | tf_op | source)
XLA Modules:
  0.0 160.1 jit_solution(11267425315163392430)
XLA Ops:
  0.0 0.0 copy-start
  0.0 3.9 %copy.12 = bf16[1,4,16,2,96,128]{5,4,2,3,0,1:T(8,128)(2,1)} copy(bf16[1,4,16,2,96,128]{5,4,3,2,1,0:T(8,128)(2,1)} %bitcast.40) | data formatting | bytes 6291456 | tf_op jit(solution)/shard_map/reshape | solution.py:61
  3.9 0.0 copy-start.1
  3.9 6.6 %all-to-all-start = ((bf16[1,4,16,2,96,128]{5,4,2,3,0,1:T(8,128)(2,1)}), bf16[1,4,16,2,96,128]{5,4,2,3,0,1:T(8,128)(2,1)}, u32[]{:S(2)}, u32[]{:S(2)}) async-start(bf16[1,4,16,2,96,128]{5,4,2,3,0,1:T(8,128)(2,1)} %copy.12), calls=%async_computation | async-start | bytes 6291456 | tf_op jit(solution)/shard_map/all_to_all | solution.py:70
  10.5 0.0 copy-done.1
  10.6 2.6 %slice.14 = bf16[1,64,192,31]{3,2,1,0:T(8,128)(2,1)} slice(bf16[1,64,192,128]{3,2,1,0:T(8,128)(2,1)S(1)} %bitcast.38), slice={[0:1], [0:64], [0:192], [97:128]} | slice | bytes 1523712 | tf_op jit(solution)/shard_map/slice | solution.py:33
  13.2 4.4 %copy.14 = bf16[1,64,192,31]{2,1,3,0:T(8,128)(2,1)} copy(bf16[1,64,192,31]{3,2,1,0:T(8,128)(2,1)} %slice.14) | data formatting | bytes 1523712 | tf_op jit(solution)/shard_map/slice | solution.py:33
  17.6 0.0 copy-start.2
  17.6 4.5 %collective-permute-start = (bf16[1,64,192,31]{2,1,3,0:T(8,128)(2,1)}, bf16[1,64,192,31]{2,1,3,0:T(8,128)(2,1)}, u32[]{:S(2)}, u32[]{:S(2)}) collective-permute-start(bf16[1,64,192,31]{2,1,3,0:T(8,128)(2,1)} %copy.14), channel_id=1, source_target_pairs={{0,2},{1,3},{4,6},{5,7},{8,10},{9,11},{12,14},{13,15},{16,18},{17,... | collective-permute-start | bytes 2285576 | tf_op jit(solution)/shard_map/ppermute | solution.py:14
  22.1 4.8 %copy.16 = bf16[1,64,192,128]{2,3,1,0:T(8,128)(2,1)} copy(bf16[1,64,192,128]{3,2,1,0:T(8,128)(2,1)S(1)} %bitcast.39) | data formatting | bytes 6291456 | tf_op jit(solution)/shard_map/reshape | solution.py:30
  27.6 0.0 copy-done
  27.6 0.0 copy-done.2
  27.6 1.1 convolution_convert_fusion
  28.7 14.2 %collective-permute-done = bf16[1,64,192,31]{2,1,3,0:T(8,128)(2,1)} collective-permute-done((bf16[1,64,192,31]{2,1,3,0:T(8,128)(2,1)}, bf16[1,64,192,31]{2,1,3,0:T(8,128)(2,1)}, u32[]{:S(2)}, u32[]{:S(2)}) %collective-permute-start) | collective-permute-done | bytes 761888 | tf_op jit(solution)/shard_map/ppermute | solution.py:14
  42.9 1.8 %copy.15 = bf16[1,64,192,31]{2,3,1,0:T(8,128)(2,1)S(1)} copy(bf16[1,64,192,31]{2,1,3,0:T(8,128)(2,1)} %collective-permute-done) | data formatting | bytes 1523712 | tf_op jit(solution)/shard_map/ppermute | solution.py:14
  44.7 8.7 %fusion.14 = bf16[64,192,128]{2,1,0:T(8,128)(2,1)} fusion(bf16[64,159,128]{2,0,1:T(8,128)(2,1)S(1)} %convolution_convert_fusion, bf16[1,64,192,128]{2,3,1,0:T(8,128)(2,1)} %copy.16, bf16[1,64,192,31]{2,3,1,0:T(8,128)(2,1)S(1)} %copy.15), kind=kOutput, calls=%fused_computation.16 | convolution fusion | flops 509558784 | bytes 9658368 | tf_op jit(solution)/shard_map/scanj,scju->scanu/dot_general | solution.py:50
  53.4 27.9 %all-to-all-done = bf16[1,4,16,2,96,128]{5,4,2,3,0,1:T(8,128)(2,1)} async-done(((bf16[1,4,16,2,96,128]{5,4,2,3,0,1:T(8,128)(2,1)}), bf16[1,4,16,2,96,128]{5,4,2,3,0,1:T(8,128)(2,1)}, u32[]{:S(2)}, u32[]{:S(2)}) %all-to-all-start) | async-done | bytes 3145760 | tf_op jit(solution)/shard_map/all_to_all | solution.py:70
  81.3 3.7 %all-to-all-start.1 = ((bf16[1,4,16,192,128]{4,3,2,0,1:T(8,128)(2,1)}), bf16[1,4,16,192,128]{4,3,2,0,1:T(8,128)(2,1)S(1)}, u32[]{:S(2)}, u32[]{:S(2)}) async-start(bf16[1,4,16,192,128]{4,3,2,0,1:T(8,128)(2,1)} %bitcast.10), calls=%async_computation.1 | async-start | bytes 6291456 | tf_op jit(solution)/shard_map/all_to_all | solution.py:69
  85.0 2.3 %copy.32 = bf16[1,4,16,2,96,128]{5,4,1,2,3,0:T(8,128)(2,1)S(1)} copy(bf16[1,4,16,2,96,128]{5,4,2,3,0,1:T(8,128)(2,1)} %all-to-all-done) | data formatting | bytes 6291456 | tf_op jit(solution)/shard_map/all_to_all | solution.py:70
  87.3 1.4 fusion.27
  88.7 2.0 %slice_bitcast_fusion = (bf16[4,16,96,128]{3,2,0,1:T(8,128)(2,1)}, bf16[4,16,96,128]{3,2,0,1:T(8,128)(2,1)}) fusion(bf16[4,16,2,96,128]{4,3,0,1,2:T(8,128)(2,1)S(1)} %bitcast.37), kind=kLoop, calls=%fused_computation.19 | loop fusion | bytes 6291456 | tf_op jit(solution)/shard_map/squeeze | solution.py:19
  90.7 64.4 %all-to-all-done.1 = bf16[1,4,16,192,128]{4,3,2,0,1:T(8,128)(2,1)S(1)} async-done(((bf16[1,4,16,192,128]{4,3,2,0,1:T(8,128)(2,1)}), bf16[1,4,16,192,128]{4,3,2,0,1:T(8,128)(2,1)S(1)}, u32[]{:S(2)}, u32[]{:S(2)}) %all-to-all-start.1) | async-done | bytes 3145760 | tf_op jit(solution)/shard_map/all_to_all | solution.py:69
  155.1 4.9 %bitcast_convert_fusion = bf16[16,256,128]{2,1,0:T(8,128)(2,1)} fusion(bf16[1,4,16,192,128]{4,3,2,0,1:T(8,128)(2,1)S(1)} %all-to-all-done.1, bf16[4,16,96,128]{3,2,0,1:T(8,128)(2,1)} %get-tuple-element.6, bf16[4,16,96,128]{3,2,0,1:T(8,128)(2,1)} %fusion.27, bf16[4,16,96,128]{3,2,0,1:T(8,128)(2,1)} %get-tuple-element.5), kind=kOutput, calls=%fused_computation.17 | convolution fusion | flops 830996480 | bytes 8912896 | tf_op jit(solution)/shard_map/scan,scat->cnt/dot_general | solution.py:71
  (2 shorter events, 0.0 us)
Async XLA Ops:
  0.0 27.6 %copy-start = (bf16[16,16]{1,0:T(8,128)(2,1)S(1)}, bf16[16,16]{1,0:T(8,128)(2,1)}, u32[]{:S(2)}) copy-start(bf16[16,16]{1,0:T(8,128)(2,1)} %param.8) | copy-start | bytes 1540
  3.9 6.6 %copy-start.1 = (bf16[1,64,2,96,128]{4,3,2,1,0:T(8,128)(2,1)S(1)}, bf16[1,64,2,96,128]{4,3,2,1,0:T(8,128)(2,1)}, u32[]{:S(2)}) copy-start(bf16[1,64,2,96,128]{4,3,2,1,0:T(8,128)(2,1)} %param.5) | copy-start | bytes 9437188
  3.9 77.4 %all-to-all-start = ((bf16[1,4,16,2,96,128]{5,4,2,3,0,1:T(8,128)(2,1)}), bf16[1,4,16,2,96,128]{5,4,2,3,0,1:T(8,128)(2,1)}, u32[]{:S(2)}, u32[]{:S(2)}) async-start(bf16[1,4,16,2,96,128]{5,4,2,3,0,1:T(8,128)(2,1)} %copy.12), calls=%async_computation | async-start | bytes 6291456 | tf_op jit(solution)/shard_map/all_to_all | solution.py:70
  17.6 10.0 %copy-start.2 = (s32[1,64]{1,0:T(1,128)S(1)}, s32[1,64]{1,0:T(1,128)}, u32[]{:S(2)}) copy-start(s32[1,64]{1,0:T(1,128)} %param.7) | copy-start | bytes 772
  17.6 25.3 %collective-permute-start = (bf16[1,64,192,31]{2,1,3,0:T(8,128)(2,1)}, bf16[1,64,192,31]{2,1,3,0:T(8,128)(2,1)}, u32[]{:S(2)}, u32[]{:S(2)}) collective-permute-start(bf16[1,64,192,31]{2,1,3,0:T(8,128)(2,1)} %copy.14), channel_id=1, source_target_pairs={{0,2},{1,3},{4,6},{5,7},{8,10},{9,11},{12,14},{13,15},{16,18},{17,... | collective-permute-start | bytes 2285576 | tf_op jit(solution)/shard_map/ppermute | solution.py:14
  81.3 73.8 %all-to-all-start.1 = ((bf16[1,4,16,192,128]{4,3,2,0,1:T(8,128)(2,1)}), bf16[1,4,16,192,128]{4,3,2,0,1:T(8,128)(2,1)S(1)}, u32[]{:S(2)}, u32[]{:S(2)}) async-start(bf16[1,4,16,192,128]{4,3,2,0,1:T(8,128)(2,1)} %bitcast.10), calls=%async_computation.1 | async-start | bytes 6291456 | tf_op jit(solution)/shard_map/all_to_all | solution.py:69
where the time goes:
time: 161 us; the launch traced here: 160 us
  waiting for transfers between devices  107 us (66%)
  local copies, waits for them, and re-layouts  21.9 us (14%)
  starting transfers between devices  14.8 us (9%)
  matrix products  14.7 us (9%)
    all_to_all x1, waiting for transfers between devices, body(): lax.all_to_all(split_in, 'station', split_axis=1, concat_axis=0, tiled=True)  64.4 us
    all_to_all x1, waiting for transfers between devices, body(): lax.all_to_all(split_steer, 'station', split_axis=1, concat_axis=0, tiled...  27.9 us
    ppermute x1, waiting for transfers between devices, passed_along(): lax.ppermute(value, axis, [(source, source + steps) for source in range(l...  14.2 us
    dot_general x1, matrix products, body(): jnp.einsum('scanj,scju->scanu', windows, band_matrix, preferred_element_t...  8.68 us
    slice x2, local copies, waits for them, and re-layouts, body(): flat_voltages[..., time_length - halo_len:]  7.05 us
    all_to_all x1, starting transfers between devices, body(): lax.all_to_all(split_steer, 'station', split_axis=1, concat_axis=0, tiled...  6.61 us
    dot_general x1, matrix products, body(): jnp.einsum('scan,scat->cnt', steering_matrix(gathered_w[:, 0]), gathered_...  4.93 us
    reshape x1, local copies, waits for them, and re-layouts, body(): voltages.reshape(station_number, channel_total, pairing_total * antenna_t...  4.84 us
  transfers between devices with their start and end apart: 3, of which 3 were waited for; matrix products, arithmetic and copies ran while one was open for 18% of the time, Pallas kernels for 0%

commit v1 on v0

v1 whole, which is shorter than its diff:
```python
import functools

import jax
import jax.numpy as jnp
from jax import lax
from jax.experimental import pallas as pl
from jax.experimental.pallas import tpu as pltpu
from jax.sharding import PartitionSpec as P

MAXD = 16
MESH = pl.DeviceIdType.MESH
CHUNK = 2


def kernel(
    n, tm_count, sizes, tap_sets, delays, taps, v_hbm, w_hbm, out_buf,
    v_buf, w_buf, band, halo_out, halo_in, acc_out, acc_in,
    v_sem, w_sem, hs_sem, hr_sem, as_sem, ar_sem,
):
    channels, parts, antennas, beams, time_len, chunk, pad = sizes
    rows = channels // n
    half = rows // 2
    per_half = half // chunk
    rows_in = parts * antennas
    folds = time_len // pad
    fold_rows = rows_in // folds
    set_count, tap_count = taps.shape
    items = n * per_half

    me = lax.axis_index("station")
    tm = lax.axis_index("tm")
    right, left = lax.rem(me + 1, n), lax.rem(me + n - 1, n)
    later, earlier = lax.rem(tm + 1, tm_count), lax.rem(tm + tm_count - 1, tm_count)

    def place(it, side):
        step, k = it // per_half, lax.rem(it, per_half)
        odd = lax.rem(step, 2)
        offset = n // 2 - odd - step // 2
        if side == 0:
            block, second = lax.rem(me + offset, n), odd
        else:
            block, second = lax.rem(me + n - offset, n), 1 - odd
        within = second * half + k * chunk
        return block * rows + within, within

    def v_copy(it, side):
        first, _ = place(it, side)
        span = pl.ds(first, chunk)
        return pltpu.make_async_copy(v_hbm.at[span], v_buf.at[span], v_sem.at[it, side])

    def w_copy(it, side):
        first, _ = place(it, side)
        span = pl.ds(first, chunk)
        return pltpu.make_async_copy(w_hbm.at[span], w_buf.at[span], w_sem.at[it, side])

    def halo_copy(it, side):
        return pltpu.make_async_remote_copy(
            src_ref=halo_out.at[it, side],
            dst_ref=halo_in.at[it, side],
            send_sem=hs_sem.at[it, side],
            recv_sem=hr_sem.at[it, side],
            device_id={"tm": later},
            device_id_type=MESH,
        )

    def sum_copy(it, side):
        return pltpu.make_async_remote_copy(
            src_ref=acc_out.at[it, side],
            dst_ref=acc_in.at[it, side],
            send_sem=as_sem.at[it, side],
            recv_sem=ar_sem.at[it, side],
            device_id={"station": right if side == 0 else left},
            device_id_type=MESH,
        )

    def start_loads(it, carry):
        for side in (0, 1):
            v_copy(it, side).start()
            w_copy(it, side).start()
        return carry

    lax.fori_loop(0, items, start_loads, 0)

    barrier = pltpu.get_barrier_semaphore()
    for target in ({"station": left}, {"station": right}, {"tm": earlier}, {"tm": later}):
        pl.semaphore_signal(barrier, inc=1, device_id=target, device_id_type=MESH)

    from_row = lax.broadcasted_iota(jnp.int32, (folds * time_len, time_len), 0)
    to_lane = lax.broadcasted_iota(jnp.int32, (folds * time_len, time_len), 1)
    wanted = (to_lane // pad) * time_len + lax.rem(to_lane, pad) + time_len - pad
    picker = (from_row == wanted).astype(jnp.float32).astype(jnp.bfloat16)

    def pack(it, side):
        first, _ = place(it, side)
        v_copy(it, side).wait()
        for c in range(chunk):
            wide = jnp.concatenate(
                [v_buf[first + c, pl.ds(q * fold_rows, fold_rows), :] for q in range(folds)], axis=1
            )
            halo_out[it, side, c] = jnp.dot(
                wide, picker, preferred_element_type=jnp.float32
            ).astype(jnp.bfloat16)
        halo_copy(it, side).start()

    pl.semaphore_wait(barrier, 4)

    def pack_first(it, carry):
        pack(it, 0)
        pack(it, 1)
        return carry

    lead = per_half
    lax.fori_loop(0, lead, pack_first, 0)

    out_pos = lax.broadcasted_iota(jnp.int32, (time_len, 2 * time_len), 0)
    column = lax.broadcasted_iota(jnp.int32, (time_len, 2 * time_len), 1)
    in_pos = jnp.where(column < time_len, column, lax.rem(column, pad) - pad)
    usable = (column < time_len) | (tm > 0)
    lag = jnp.where(usable, out_pos - delays[0] - in_pos, -1)

    def make_band(m, carry):
        values = jnp.zeros((time_len, 2 * time_len), jnp.float32)
        for k in range(tap_count):
            values = jnp.where(lag == k, taps[m, k], values)
        band[m] = values.astype(jnp.bfloat16)
        return carry

    lax.fori_loop(0, set_count, make_band, 0)

    fold_lane = lax.broadcasted_iota(jnp.int32, (fold_rows, time_len), 1) // pad

    def beams_of(it, side, c):
        first, _ = place(it, side)
        channel = first + c
        rim = halo_in[it, side, c]
        rims = jnp.concatenate(
            [jnp.where(fold_lane == q, rim, jnp.zeros_like(rim)) for q in range(folds)], axis=0
        )
        window = jnp.concatenate([v_buf[channel], rims], axis=1)
        filt = band[tap_sets[0, channel]]
        delayed = lax.dot_general(
            filt, window, (((1,), (1,)), ((), ())), preferred_element_type=jnp.float32
        ).astype(jnp.bfloat16)
        wr = w_buf[channel, pl.ds(0, antennas), :]
        wi = w_buf[channel, pl.ds(antennas, antennas), :]
        steer = jnp.concatenate(
            [jnp.concatenate([wr, wi], axis=1), jnp.concatenate([-wi, wr], axis=1)], axis=0
        )
        return jnp.dot(delayed, steer, preferred_element_type=jnp.float32)

    def ready(it, side):
        halo_copy(it, side).wait_recv()
        w_copy(it, side).wait()

    def head(it, carry):
        for side in (0, 1):
            pack(it + lead, side)
        for side in (0, 1):
            ready(it, side)
            for c in range(chunk):
                acc_out[it, side, c] = beams_of(it, side, c).astype(jnp.bfloat16)
            sum_copy(it, side).start()
        return carry

    lax.fori_loop(0, 2 * per_half, head, 0)

    def middle(it, carry):
        for side in (0, 1):
            pack(it + lead, side)
        for side in (0, 1):
            ready(it, side)
            before = it - 2 * per_half
            sum_copy(before, side).wait_recv()
            for c in range(chunk):
                total = beams_of(it, side, c) + acc_in[before, side, c].astype(jnp.float32)
                acc_out[it, side, c] = total.astype(jnp.bfloat16)
            sum_copy(it, side).start()
        return carry

    lax.fori_loop(2 * per_half, items - per_half, middle, 0)

    def last(it, carry):
        for side in (0, 1):
            ready(it, side)
            _, within = place(it, side)
            same, other = it - 2 * per_half, it - per_half
            sums = [beams_of(it, side, c) for c in range(chunk)]
            sum_copy(same, side).wait_recv()
            sum_copy(other, 1 - side).wait_recv()
            for c in range(chunk):
                total = sums[c] + acc_in[same, side, c].astype(jnp.float32)
                total = total + acc_in[other, 1 - side, c].astype(jnp.float32)
                out_buf[within + c] = total.T.astype(jnp.bfloat16)
        return carry

    lax.fori_loop(items - per_half, items, last, 0)

    def drain_halo(it, carry):
        for side in (0, 1):
            halo_copy(it, side).wait_send()
        return carry

    lax.fori_loop(0, items, drain_halo, 0)

    def drain_sums(it, carry):
        for side in (0, 1):
            sum_copy(it, side).wait_send()
        return carry

    lax.fori_loop(0, items - per_half, drain_sums, 0)


def body(voltages, delays, tap_sets, tap_table, weights):
    _, channels, parts, antennas, time_len = voltages.shape
    beams = weights.shape[-1]
    set_count, tap_count = tap_table.shape
    n = lax.axis_size("station")
    tm_count = lax.axis_size("tm")
    rows = channels // n
    chunk = min(CHUNK, rows // 2)
    per_half = rows // 2 // chunk
    items = n * per_half
    pad = MAXD + tap_count
    rows_in = parts * antennas
    fold_rows = rows_in * pad // time_len
    sizes = (channels, parts, antennas, beams, time_len, chunk, pad)
    sent = items - per_half
    bf16 = jnp.bfloat16
    dma = pltpu.SemaphoreType.DMA
    smem = pl.BlockSpec(memory_space=pltpu.SMEM)
    in_hbm = pl.BlockSpec(memory_space=pltpu.HBM)
    result = pl.pallas_call(
        functools.partial(kernel, n, tm_count, sizes),
        out_shape=jax.ShapeDtypeStruct((rows, 2 * beams, time_len), bf16),
        in_specs=[smem, smem, smem, in_hbm, in_hbm],
        out_specs=pl.BlockSpec(memory_space=pltpu.VMEM),
        scratch_shapes=[
            pltpu.VMEM((channels, rows_in, time_len), bf16),
            pltpu.VMEM((channels, rows_in, beams), bf16),
            pltpu.VMEM((set_count, time_len, 2 * time_len), bf16),
            pltpu.VMEM((items, 2, chunk, fold_rows, time_len), bf16),
            pltpu.VMEM((items, 2, chunk, fold_rows, time_len), bf16),
            pltpu.VMEM((sent, 2, chunk, time_len, 2 * beams), bf16),
            pltpu.VMEM((sent, 2, chunk, time_len, 2 * beams), bf16),
            dma((items, 2)),
            dma((items, 2)),
            dma((items, 2)),
            dma((items, 2)),
            dma((sent, 2)),
            dma((sent, 2)),
        ],
        compiler_params=pltpu.CompilerParams(
            collective_id=0, has_side_effects=True, vmem_limit_bytes=48 * 1024 * 1024
        ),
    )(
        tap_sets,
        delays,
        tap_table.astype(jnp.float32),
        voltages.reshape(channels, rows_in, time_len),
        weights.reshape(channels, rows_in, beams),
    )
    return result.reshape(rows, 2, beams, time_len)


def solution(mesh):
    return jax.shard_map(
        body,
        mesh=mesh,
        in_specs=(
            P(("group", "station"), "chan", None, None, "tm"),
            P(("group", "station")),
            P(("group", "station"), "chan"),
            P(),
            P(("group", "station"), "chan", None, None, None),
        ),
        out_specs=P(("group", "chan", "station"), None, None, "tm"),
        check_vma=False,
    )
```

time: 161 us -> 90.3 us (0.56)
  waiting for transfers between devices: 107 us -> 0 us
  Pallas kernels: 0 us -> 85.3 us
  local copies, waits for them, and re-layouts: 21.9 us -> 3.52 us
  starting transfers between devices: 14.8 us -> 0 us
  matrix products: 14.7 us -> 0 us
    all_to_all x2 -> x0, waiting for transfers between devices: 92.4 us -> none  [the longest x1 64.4 us: body(): lax.all_to_all(split_in, 'station', split_axis=1, concat_axis=0, tiled=True)]
    pallas_call x0 -> x1, Pallas kernels: none -> 85.3 us  [body(): pl.pallas_call(functools.partial(kernel, n, tm_count, sizes), out_shape=j...]
    dot_general x3 -> x0, matrix products: 14.7 us -> none  [the longest x1 8.68 us: body(): jnp.einsum('scanj,scju->scanu', windows, band_matrix, preferred_element_t...]
    ppermute x1 -> x0, waiting for transfers between devices: 14.2 us -> none  [passed_along(): lax.ppermute(value, axis, [(source, source + steps) for source in range(l...]
    all_to_all x2 -> x0, starting transfers between devices: 10.3 us -> none  [the longest x1 6.61 us: body(): lax.all_to_all(split_steer, 'station', split_axis=1, concat_axis=0, tiled...]
    reshape x2 -> x0, local copies, waits for them, and re-layouts: 8.77 us -> none  [the longest x1 4.84 us: body(): voltages.reshape(station_number, channel_total, pairing_total * antenna_t...]
    slice x2 -> x0, local copies, waits for them, and re-layouts: 7.05 us -> none  [body(): flat_voltages[..., time_length - halo_len:]]
    ppermute x1 -> x0, starting transfers between devices: 4.49 us -> none  [passed_along(): lax.ppermute(value, axis, [(source, source + steps) for source in range(l...]
  transfers between devices with their start and end apart: 3 -> 0, of which waited for: 3 -> 0; matrix products, arithmetic and copies ran while one was open for 18% -> 0% of each run, Pallas kernels for 0% -> 0%
where the time goes in v1:
time: 90.3 us; the launch traced here: 90.2 us
  Pallas kernels  85.3 us (94%)
  local copies, waits for them, and re-layouts  3.52 us (4%)
    pallas_call x1, Pallas kernels, body(): pl.pallas_call(functools.partial(kernel, n, tm_count, sizes), out_shape=j...  85.3 us
    unnamed x5, local copies, waits for them, and re-layouts  3.52 us

profile of v1, /device:TPU:0, one launch (start us, length us, event | category | flops | bytes accessed | tf_op | source)
XLA Modules:
  0.0 90.2 jit_solution(17655543318121796924)
XLA Ops:
  0.7 0.7 convert_element_type.3.taps
  1.3 0.0 copy-start
  1.3 1.9 %copy-done = bf16[1,64,2,96,128]{4,3,2,1,0:T(8,128)(2,1)S(1)} copy-done((bf16[1,64,2,96,128]{4,3,2,1,0:T(8,128)(2,1)S(1)}, bf16[1,64,2,96,128]{4,3,2,1,0:T(8,128)(2,1)}, u32[]{:S(2)}) %copy-start) | copy-done | bytes 3145752
  3.2 0.0 copy-start.1
  3.2 0.7 copy-done.1
  3.9 85.3 %shard_map.55 = bf16[16,256,128]{2,1,0:T(8,128)(2,1)S(1)} custom-call(s32[1,64]{1,0:T(1,128)S(1)} %copy-done.1, s32[1]{0:T(128)S(6)} %copy.7.delays, f32[16,16]{1,0:T(8,128)S(1)} %convert_element_type.3.taps, bf16[64,192,128]{2,1,0:T(8,128)(2,1)S(1)} %bitcast.4, bf16[64,192,128]{2,1,0:T(8,128)(2,1)} %bitcast.5), custom_call_target="tpu_custom_call" | custom-call | tf_op jit(solution)/shard_map/pallas_call | solution.py:232
  89.2 1.0 %copy.8 = bf16[16,2,128,128]{3,2,1,0:T(8,128)(2,1)} copy(bf16[16,2,128,128]{3,2,1,0:T(8,128)(2,1)S(1)} %bitcast.3) | data formatting | bytes 2097152
Async XLA Ops:
  1.3 1.9 %copy-start = (bf16[1,64,2,96,128]{4,3,2,1,0:T(8,128)(2,1)S(1)}, bf16[1,64,2,96,128]{4,3,2,1,0:T(8,128)(2,1)}, u32[]{:S(2)}) copy-start(bf16[1,64,2,96,128]{4,3,2,1,0:T(8,128)(2,1)} %param.5) | copy-start | bytes 9437188
  3.2 0.7 copy-start.1

commit v2 on v1

v2 whole, which is shorter than its diff:
```python
import functools

import jax
import jax.numpy as jnp
from jax import lax
from jax.experimental import pallas as pl
from jax.experimental.pallas import tpu as pltpu
from jax.sharding import PartitionSpec as P

MAXD = 16
MESH = pl.DeviceIdType.MESH
CHUNK = 8
LEAD = 2


def kernel(
    n, tm_count, sizes, tap_sets, delays, taps, v_hbm, w_hbm, out_buf,
    v_buf, w_buf, band, tap_values, halo_out, halo_in, own_sum, acc_out, acc_in,
    v_sem, w_sem, hs_sem, hr_sem, as_sem, ar_sem,
):
    channels, parts, antennas, beams, time_len, chunk, pad = sizes
    rows = channels // n
    per_block = rows // chunk
    rows_in = parts * antennas
    folds = time_len // pad
    fold_rows = rows_in // folds
    set_count, tap_count = taps.shape
    sends = (n - 1) * per_block
    items = n * per_block

    me = lax.axis_index("station")
    tm = lax.axis_index("tm")
    right, left = lax.rem(me + 1, n), lax.rem(me + n - 1, n)
    later, earlier = lax.rem(tm + 1, tm_count), lax.rem(tm + tm_count - 1, tm_count)

    def place(it, side):
        step, k = it // per_block, lax.rem(it, per_block)
        own = step // (n - 1)
        if side == 0:
            block = (1 - own) * (n - 1 - step) + own * me
            valid = (n - 1 - step > me) | (step == n - 1)
        else:
            block, valid = step, step < me
        return block * per_block + k, valid

    def v_copy(at):
        span = pl.ds(at * chunk, chunk)
        return pltpu.make_async_copy(v_hbm.at[span], v_buf.at[span], v_sem.at[at])

    def w_copy(at):
        span = pl.ds(at * chunk, chunk)
        return pltpu.make_async_copy(w_hbm.at[span], w_buf.at[span], w_sem.at[at])

    def halo_copy(at):
        return pltpu.make_async_remote_copy(
            src_ref=halo_out.at[at],
            dst_ref=halo_in.at[at],
            send_sem=hs_sem.at[at],
            recv_sem=hr_sem.at[at],
            device_id={"tm": later},
            device_id_type=MESH,
        )

    def sum_copy(it, side):
        return pltpu.make_async_remote_copy(
            src_ref=acc_out.at[it, side],
            dst_ref=acc_in.at[it, side],
            send_sem=as_sem.at[it, side],
            recv_sem=ar_sem.at[it, side],
            device_id={"station": right if side == 0 else left},
            device_id_type=MESH,
        )

    def each(start, stop, act):
        def one(it, carry):
            for side in (0, 1):
                at, valid = place(it, side)

                @pl.when(valid)
                def _(at=at, side=side):
                    act(it, side, at)

            return carry

        lax.fori_loop(start, stop, one, 0)

    def start_loads(it, side, at):
        v_copy(at).start()
        w_copy(at).start()

    each(0, items, start_loads)

    barrier = pltpu.get_barrier_semaphore()
    for target in ({"station": left}, {"station": right}, {"tm": earlier}, {"tm": later}):
        pl.semaphore_signal(barrier, inc=1, device_id=target, device_id_type=MESH)

    from_row = lax.broadcasted_iota(jnp.int32, (folds * time_len, time_len), 0)
    to_lane = lax.broadcasted_iota(jnp.int32, (folds * time_len, time_len), 1)
    wanted = (to_lane // pad) * time_len + lax.rem(to_lane, pad) + time_len - pad
    picker = (from_row == wanted).astype(jnp.float32).astype(jnp.bfloat16)

    def pack(it, side, at):
        v_copy(at).wait()
        for c in range(chunk):
            wide = jnp.concatenate(
                [v_buf[at * chunk + c, pl.ds(q * fold_rows, fold_rows), :] for q in range(folds)], axis=1
            )
            halo_out[at, c] = jnp.dot(
                wide, picker, preferred_element_type=jnp.float32
            ).astype(jnp.bfloat16)
        halo_copy(at).start()

    pl.semaphore_wait(barrier, 4)

    lead = min(LEAD, per_block)
    each(0, lead, pack)

    out_pos = lax.broadcasted_iota(jnp.int32, (time_len, 2 * time_len), 0)
    column = lax.broadcasted_iota(jnp.int32, (time_len, 2 * time_len), 1)
    in_pos = jnp.where(column < time_len, column, lax.rem(column, pad) - pad)
    usable = (column < time_len) | (tm > 0)
    lag = jnp.where(usable, out_pos - delays[0] - in_pos, -1)
    tap_values[...] = taps[...].astype(jnp.float32)

    def make_band(m, carry):
        row = tap_values[pl.ds(m, 1), :]
        values = jnp.zeros((time_len, 2 * time_len), jnp.float32)
        for k in range(tap_count):
            values = jnp.where(lag == k, row[:, k : k + 1], values)
        band[m] = values.astype(jnp.bfloat16)
        return carry

    lax.fori_loop(0, set_count, make_band, 0)

    fold_lane = lax.broadcasted_iota(jnp.int32, (fold_rows, time_len), 1) // pad

    def beams_of(at, c):
        channel = at * chunk + c
        rim = halo_in[at, c]
        rims = jnp.concatenate(
            [jnp.where(fold_lane == q, rim, jnp.zeros_like(rim)) for q in range(folds)], axis=0
        )
        window = jnp.concatenate([v_buf[channel], rims], axis=1)
        filt = band[tap_sets[0, channel]]
        delayed = lax.dot_general(
            filt, window, (((1,), (1,)), ((), ())), preferred_element_type=jnp.float32
        ).astype(jnp.bfloat16)
        wr = w_buf[channel, pl.ds(0, antennas), :]
        wi = w_buf[channel, pl.ds(antennas, antennas), :]
        steer = jnp.concatenate(
            [jnp.concatenate([wr, wi], axis=1), jnp.concatenate([-wi, wr], axis=1)], axis=0
        )
        return jnp.dot(delayed, steer, preferred_element_type=jnp.float32)

    def compute(at):
        halo_copy(at).wait_recv()
        w_copy(at).wait()
        for c in range(chunk):
            own_sum[c] = beams_of(at, c)

    def send(it, side, at):
        compute(at)
        first = me == (0 if side == 0 else n - 1)

        @pl.when(first)
        def _():
            for c in range(chunk):
                acc_out[it, side, c] = own_sum[c].astype(jnp.bfloat16)

        @pl.when(jnp.logical_not(first))
        def _():
            sum_copy(it, side).wait_recv()
            for c in range(chunk):
                total = own_sum[c] + acc_in[it, side, c].astype(jnp.float32)
                acc_out[it, side, c] = total.astype(jnp.bfloat16)

        sum_copy(it, side).start()

    def send_step(it, carry):
        each(it + lead, it + lead + 1, pack)
        each(it, it + 1, send)
        return carry

    lax.fori_loop(0, sends, send_step, 0)

    def last(k, carry):
        at = me * per_block + k

        @pl.when(k + lead < per_block)
        def _():
            pack(0, 0, at + lead)

        compute(at)

        @pl.when(me < n - 1)
        def _():
            slot = me * per_block + k
            sum_copy(slot, 1).wait_recv()
            for c in range(chunk):
                own_sum[c] += acc_in[slot, 1, c].astype(jnp.float32)

        @pl.when(me > 0)
        def _():
            slot = (n - 1 - me) * per_block + k
            sum_copy(slot, 0).wait_recv()
            for c in range(chunk):
                own_sum[c] += acc_in[slot, 0, c].astype(jnp.float32)

        for c in range(chunk):
            out_buf[k * chunk + c] = own_sum[c].T.astype(jnp.bfloat16)
        return carry

    lax.fori_loop(0, per_block, last, 0)

    each(0, items, lambda it, side, at: halo_copy(at).wait_send())
    each(0, sends, lambda it, side, at: sum_copy(it, side).wait_send())


def body(voltages, delays, tap_sets, tap_table, weights):
    _, channels, parts, antennas, time_len = voltages.shape
    beams = weights.shape[-1]
    set_count, tap_count = tap_table.shape
    n = lax.axis_size("station")
    tm_count = lax.axis_size("tm")
    rows = channels // n
    chunk = min(CHUNK, rows)
    items = channels // chunk
    pad = MAXD + tap_count
    rows_in = parts * antennas
    fold_rows = rows_in * pad // time_len
    sizes = (channels, parts, antennas, beams, time_len, chunk, pad)
    sent = items - rows // chunk
    bf16 = jnp.bfloat16
    dma = pltpu.SemaphoreType.DMA
    smem = pl.BlockSpec(memory_space=pltpu.SMEM)
    in_hbm = pl.BlockSpec(memory_space=pltpu.HBM)
    result = pl.pallas_call(
        functools.partial(kernel, n, tm_count, sizes),
        out_shape=jax.ShapeDtypeStruct((rows, 2 * beams, time_len), bf16),
        in_specs=[smem, smem, pl.BlockSpec(memory_space=pltpu.VMEM), in_hbm, in_hbm],
        out_specs=pl.BlockSpec(memory_space=pltpu.VMEM),
        scratch_shapes=[
            pltpu.VMEM((channels, rows_in, time_len), bf16),
            pltpu.VMEM((channels, rows_in, beams), bf16),
            pltpu.VMEM((set_count, time_len, 2 * time_len), bf16),
            pltpu.VMEM((set_count, tap_count), jnp.float32),
            pltpu.VMEM((items, chunk, fold_rows, time_len), bf16),
            pltpu.VMEM((items, chunk, fold_rows, time_len), bf16),
            pltpu.VMEM((chunk, time_len, 2 * beams), jnp.float32),
            pltpu.VMEM((sent, 2, chunk, time_len, 2 * beams), bf16),
            pltpu.VMEM((sent, 2, chunk, time_len, 2 * beams), bf16),
            dma((items,)),
            dma((items,)),
            dma((items,)),
            dma((items,)),
            dma((sent, 2)),
            dma((sent, 2)),
        ],
        compiler_params=pltpu.CompilerParams(
            collective_id=0, has_side_effects=True, vmem_limit_bytes=60 * 1024 * 1024
        ),
    )(
        tap_sets,
        delays,
        tap_table,
        voltages.reshape(channels, rows_in, time_len),
        weights.reshape(channels, rows_in, beams),
    )
    return result.reshape(rows, 2, beams, time_len)


def solution(mesh):
    return jax.shard_map(
        body,
        mesh=mesh,
        in_specs=(
            P(("group", "station"), "chan", None, None, "tm"),
            P(("group", "station")),
            P(("group", "station"), "chan"),
            P(),
            P(("group", "station"), "chan", None, None, None),
        ),
        out_specs=P(("group", "chan", "station"), None, None, "tm"),
        check_vma=False,
    )
```

time: 90.3 us -> 97.6 us (1.081)
  the two profiles are of different devices: /device:TPU:0 before, /device:TPU:10 now
where the time goes in v2:
time: 97.6 us; the launch traced here: 97.4 us
  Pallas kernels  94.5 us (97%)
  local copies, waits for them, and re-layouts  2.31 us (2%)
    pallas_call x1, Pallas kernels, body(): pl.pallas_call(functools.partial(kernel, n, tm_count, sizes), out_shape=j...  94.5 us
    unnamed x1, local copies, waits for them, and re-layouts  2.31 us

profile of v2, /device:TPU:10, one launch (start us, length us, event | category | flops | bytes accessed | tf_op | source)
XLA Modules:
  0.0 97.4 jit_solution(17331534701443472563)
XLA Ops:
  0.7 94.5 %shard_map.55 = bf16[16,256,128]{2,1,0:T(8,128)(2,1)} custom-call(s32[1,64]{1,0:T(1,128)} %tap_sets.1, s32[1]{0:T(128)S(6)} %copy.7.delays, bf16[16,16]{1,0:T(8,128)(2,1)} %taps.1, bf16[64,192,128]{2,1,0:T(8,128)(2,1)} %bitcast.4, bf16[64,192,128]{2,1,0:T(8,128)(2,1)} %bitcast.5), custom_call_target="tpu_custom_call" | custom-call | tf_op jit(solution)/shard_map/pallas_call | solution.py:237
  95.1 2.3 %copy.8 = bf16[16,2,128,128]{3,2,1,0:T(8,128)(2,1)} copy(bf16[16,2,128,128]{3,2,1,0:T(8,128)(2,1)} %bitcast.3) | data formatting | bytes 2097152
